TPU v7x, 32 devices: a whole 2x2x4 slice. The times are simulated.
32 devices in a mesh: dp: 4 (over y, x), vocab: 8 (over z, core).
Axes of the slice: x: 2, y: 2, z: 4, core: 2. Of those that a mesh axis runs over, the one named last changes fastest.
Arguments:
- final_activation: bfloat16 [512, 8192], P('dp', 'vocab'), may hold values from -2000 to 2000
- output_projection_weights: bfloat16 [8192, 128256], P('dp', 'vocab'), may hold values from -0.0625 to 0.0625
- context_word_tallies: int32 [512, 128256], P('dp', 'vocab'), may hold values from 0 to 2
- emitted_word_tallies: int32 [512, 128256], P('dp', 'vocab'), may hold values from 0 to 2
- freshest_word: int32 [512], P('dp'), may hold values from 0 to 128255
- recurrence_divisor: float32 [512], P('dp'), may hold values from 1.1 to 2.5
- recurrence_fine: float32 [512], P('dp'), may hold values from 0 to 1.5
- appearance_fine: float32 [512], P('dp'), may hold values from 0 to 1.5
- softness_level: float32 [512], P('dp'), may hold values from 0.5 to 2
- random_draws: float32 [512], P('dp'), may hold values from 0.02 to 0.98
Outputs:
- new_counts: int32 [512, 128256], P('dp', 'vocab')
- log_likelihoods: float32 [512, 128256], P('dp', 'vocab')
- sample_quantile: float32 [512], P('dp')
All inputs are finite; a program needn't handle non-finite values.
Results may differ from a plain program's by a relative error of at most 0.0012.
Values may be sent and summed in bfloat16 or wider, within the bound.
A program may use at most 192 MiB of HBM per device.

v0:
```python
import jax
import jax.numpy as jnp
from jax import lax
from jax.sharding import PartitionSpec as P

VOCAB = 128256


def entering(part, axis, combine, identity):
    place = lax.axis_index(axis)
    gathered = lax.all_gather(part, axis)
    state = jnp.zeros_like(part) + jnp.asarray(identity, part.dtype)

    def one(turn, state):
        return combine(state, lax.dynamic_index_in_dim(gathered, turn, 0, False))

    return lax.fori_loop(0, place, one, state)


def on_device(
    final_activation,
    output_projection_weights,
    context_word_tallies,
    emitted_word_tallies,
    freshest_word,
    recurrence_divisor,
    recurrence_fine,
    appearance_fine,
    softness_level,
    random_draws,
):
    full_rows = lax.all_gather(final_activation, "vocab", axis=1, tiled=True)
    shard_width = output_projection_weights.shape[1]
    first_id = lax.axis_index("vocab") * shard_width
    token_ids = first_id + lax.broadcasted_iota(jnp.int32, (1, shard_width), 1)
    new_counts = emitted_word_tallies + (token_ids == freshest_word[:, None]).astype(jnp.int32)
    seen = context_word_tallies + new_counts > 0
    quarter_rows = lax.all_to_all(full_rows, "dp", split_axis=1, concat_axis=0, tiled=True)
    logits = lax.psum_scatter(
        jnp.dot(quarter_rows, output_projection_weights, preferred_element_type=jnp.float32),
        "dp",
        scatter_dimension=0,
        tiled=True,
    )
    factor = recurrence_divisor[:, None]
    adjusted_scores = jnp.where(
        seen, jnp.where(logits > 0, logits / factor, logits * factor), logits
    )
    adjusted_scores = adjusted_scores - recurrence_fine[:, None] * new_counts.astype(jnp.float32)
    adjusted_scores = adjusted_scores - appearance_fine[:, None] * (new_counts > 0).astype(
        jnp.float32
    )
    softened_scores = adjusted_scores / softness_level[:, None]
    highest_score = lax.pmax(jnp.max(softened_scores, axis=1), "vocab")
    exponentiated_mass = jnp.exp(softened_scores - highest_score[:, None])
    local_sum = jnp.sum(exponentiated_mass, axis=1)
    normalizer_mass = lax.psum(local_sum, "vocab")

    def plus(earlier, later):
        return earlier + later

    lower_mass = entering(local_sum, "vocab", plus, jnp.zeros_like(local_sum))
    log_likelihoods = softened_scores - highest_score[:, None] - jnp.log(normalizer_mass)[:, None]
    probs = exponentiated_mass / normalizer_mass[:, None]
    cdf = (lower_mass / normalizer_mass)[:, None] + jnp.cumsum(probs, axis=1)
    below = cdf - probs
    taken = jnp.minimum(jnp.maximum(random_draws[:, None] - below, 0.0), probs)
    position = (token_ids.astype(jnp.float32) + 0.5) / VOCAB
    partial_quantile = jnp.sum(taken * position, axis=1)
    sample_quantile = lax.psum(partial_quantile, "vocab")
    return (new_counts, log_likelihoods, sample_quantile)


def solution(mesh):
    return jax.shard_map(
        on_device,
        mesh=mesh,
        in_specs=(
            P("dp", "vocab"),
            P("dp", "vocab"),
            P("dp", "vocab"),
            P("dp", "vocab"),
            P("dp"),
            P("dp"),
            P("dp"),
            P("dp"),
            P("dp"),
            P("dp"),
        ),
        out_specs=(P("dp", "vocab"), P("dp", "vocab"), P("dp")),
        check_vma=False,
    )
```

profile of v0, /device:TPU:0, one launch (start us, length us, event | category | flops | bytes accessed | tf_op | source)
XLA Modules:
  0.0 525.2 jit_solution(6530131259474339864)
XLA Ops:
  7.2 0.0 all-gather.4.cloned.1.call-start
  7.2 1.8 copy.21
  9.0 0.0 all-gather.4.cloned.1.call-update
  9.0 0.0 reduce-scatter.2.cloned.1.call-start
  9.1 33.0 %all-gather.4.cloned.1.call-done = bf16[128,8192]{0,1:T(8,128)(2,1)} async-done(((bf16[128,1024]{0,1:T(8,128)(2,1)}), bf16[128,8192]{0,1:T(8,128)(2,1)}) %all-gather.4.cloned.1.call-update) | async-done | bytes 2097168 | tf_op jit(solution)/shard_map/all_gather | solution.py:32
  42.1 29.6 %all_to_all.19 = bf16[128,4,2048]{0,2,1:T(8,128)(2,1)S(1)} all-to-all(bf16[128,4,2048]{0,2,1:T(8,128)(2,1)} %bitcast.19), channel_id=1, replica_groups=mesh['dp'=4,'vocab'=8] {'dp'}, dimensions={1} | all-to-all | bytes 4194304 | tf_op jit(solution)/shard_map/all_to_all | solution.py:38
  71.7 2.6 copy.22
  74.3 43.0 %fusion.10 = f32[512,16032]{0,1:T(8,128)} fusion(bf16[512,2048]{1,0:T(8,128)(2,1)} %bitcast.20, bf16[2048,16032]{0,1:T(8,128)(2,1)} %param.13), kind=kOutput, calls=%fused_computation.22 | convolution fusion | flops 33621540864 | bytes 100597760 | tf_op jit(solution)/shard_map/dot_general | solution.py:40
  117.2 0.0 copy-start.3
  117.2 0.0 copy-start.4
  117.2 0.0 copy-start.5
  117.3 0.0 copy-start.6
  117.3 0.0 copy-start.7
  117.3 0.0 reduce-scatter.2.cloned.1.call-update
  117.3 281.2 %reduce-scatter.2.cloned.1.call-done = f32[128,16032]{0,1:T(8,128)} async-done(((f32[512,16032]{0,1:T(8,128)}), f32[128,16032]{0,1:T(8,128)}) %reduce-scatter.2.cloned.1.call-update) | async-done | bytes 8208400 | tf_op jit(solution)/shard_map/reduce_scatter | solution.py:39
  398.5 0.0 copy-done.3
  398.5 0.0 copy-done.4
  398.5 0.0 copy-done.5
  398.5 0.0 copy-done.6
  398.5 0.0 copy-done.7
  398.5 16.2 %fusion.8 = (f32[128]{0:T(128)S(1)}, f32[128,16032]{0,1:T(8,128)}, s32[128,16032]{0,1:T(8,128)}) fusion(f32[128]{0:T(128)S(1)} %copy-done.3, f32[128]{0:T(128)S(1)} %copy-done.4, f32[128]{0:T(128)S(1)} %copy-done.5, f32[128,16032]{0,1:T(8,128)} %reduce-scatter.2.cloned.1.call-done, f32[128]{0:T(128)S(1)} %copy-done.6, s32[128,16032]{0,1:T(8,128)} %param.14, ...), kind=kLoop, calls=%fused_computation.20 | loop fusion | flops 36937600 | bytes 41109120 | tf_op jit(solution)/shard_map/reduce_max | solution.py:54
  414.8 16.2 %pmax.7 = f32[128]{0:T(128)S(1)} all-reduce(f32[128]{0:T(128)S(1)} %get-tuple-element.35), channel_id=1, replica_groups=mesh['dp'=4,'vocab'=8] {'vocab'}, use_global_device_ids=true, to_apply=%region_2.3 | all-reduce | flops 128 | bytes 1024 | tf_op jit(solution)/shard_map/pmax | solution.py:54
  430.9 4.5 exponential_reduce_fusion
  435.4 13.6 %psum.14 = f32[128]{0:T(128)S(1)} all-reduce(f32[128]{0:T(128)S(1)} %exponential_reduce_fusion), channel_id=1, replica_groups=mesh['dp'=4,'vocab'=8] {'vocab'}, use_global_device_ids=true, to_apply=%region_4.5 | all-reduce | flops 128 | bytes 1024 | tf_op jit(solution)/shard_map/psum | solution.py:57
  449.0 8.4 %all-gather.1 = f32[8,1,128]{2,1,0:T(1,128)S(1)} all-gather(f32[1,1,128]{2,1,0:T(1,128)S(1)} %bitcast.23), channel_id=2, replica_groups=mesh['dp'=4,'vocab'=8] {'vocab'}, dimensions={0}, use_global_device_ids=true | all-gather | bytes 4608 | tf_op jit(solution)/shard_map/all_gather | solution.py:11
  457.4 6.2 %exponential_divide_fusion = (f32[128,16032]{0,1:T(8,128)S(1)}, f32[128,16032]{0,1:T(8,128)}) fusion(f32[128,16032]{0,1:T(8,128)} %get-tuple-element.36, f32[128]{0:T(128)S(1)} %psum.14, f32[128]{0:T(128)S(1)} %pmax.7, f32[128]{0:T(128)S(1)} %get-tuple-element.41), kind=kLoop, calls=%fused_computation.13 | loop fusion | flops 6156288 | bytes 24626688 | tf_op jit(solution)/shard_map/div | solution.py:64
  463.6 0.0 copy-start
  463.6 3.6 pad.3
  467.2 2.0 copy-done
  469.2 11.4 %fusion = f32[128,126,128]{0,1,2:T(8,128)} fusion(f32[128,126,128]{0,2,1:T(8,128)} %bitcast.16), kind=kOutput, calls=%fused_computation.1 | output fusion | flops 262176768 | bytes 16515072 | tf_op jit(solution)/shard_map/reduce-window
  480.6 0.8 slice_bitcast_fusion
  481.4 0.2 reduce-window.9
  481.6 4.2 broadcast_add_fusion
  485.8 0.0 copy-start.1
  485.8 0.0 copy-start.2
  485.8 7.9 %copy.24 = f32[128,126,128]{0,2,1:T(8,128)} copy(f32[128,126,128]{0,1,2:T(8,128)S(1)} %broadcast_add_fusion) | data formatting | bytes 16515072 | tf_op jit(solution)/shard_map/reduce_window_sum
  493.8 0.0 copy-done.1
  493.8 0.0 copy-done.2
  493.8 8.3 %fusion.7 = f32[128]{0:T(128)S(1)} fusion(f32[128,16032]{0,1:T(8,128)S(1)} %copy-done.1, f32[128,16128]{0,1:T(8,128)} %bitcast.17, f32[16032]{0:T(1024)S(1)} %add_multiply_fusion, f32[128]{0:T(128)S(1)} %get-tuple-element.40, f32[128]{0:T(128)S(1)} %copy-done.2), kind=kLoop, calls=%fused_computation.9 | loop fusion | flops 14364544 | bytes 16482432 | tf_op jit(solution)/shard_map/reduce_sum | solution.py:69
  502.1 16.3 %psum.15 = f32[128]{0:T(128)} all-reduce(f32[128]{0:T(128)S(1)} %fusion.7), channel_id=1, replica_groups=mesh['dp'=4,'vocab'=8] {'vocab'}, use_global_device_ids=true, to_apply=%region_10.11 | all-reduce | flops 128 | bytes 1024 | tf_op jit(solution)/shard_map/psum | solution.py:70
  (5 shorter events, 0.0 us)
Async XLA Ops:
  7.2 34.9 %all-gather.4.cloned.1.call-start = ((), (), s32[]{:S(2)}) async-start(), calls=%async_computation.2 | async-start | bytes 2359296 | tf_op jit(solution)/shard_map/all_gather | solution.py:32
  9.0 389.5 %reduce-scatter.2.cloned.1.call-start = ((), (), s32[]{:S(2)}) async-start(), calls=%async_computation.3 | async-start | bytes 41041920 | tf_op jit(solution)/shard_map/reduce_scatter | solution.py:39
  117.2 281.3 %copy-start.3 = (f32[128]{0:T(128)S(1)}, f32[128]{0:T(128)}, u32[]{:S(2)}) copy-start(f32[128]{0:T(128)} %param.20) | copy-start | bytes 1540
  117.2 281.3 %copy-start.4 = (f32[128]{0:T(128)S(1)}, f32[128]{0:T(128)}, u32[]{:S(2)}) copy-start(f32[128]{0:T(128)} %param.19) | copy-start | bytes 1540
  117.2 281.3 %copy-start.5 = (f32[128]{0:T(128)S(1)}, f32[128]{0:T(128)}, u32[]{:S(2)}) copy-start(f32[128]{0:T(128)} %param.18) | copy-start | bytes 1540
  117.3 281.3 %copy-start.6 = (f32[128]{0:T(128)S(1)}, f32[128]{0:T(128)}, u32[]{:S(2)}) copy-start(f32[128]{0:T(128)} %param.17) | copy-start | bytes 1540
  117.3 281.3 %copy-start.7 = (s32[128]{0:T(128)S(1)}, s32[128]{0:T(128)}, u32[]{:S(2)}) copy-start(s32[128]{0:T(128)} %param.16) | copy-start | bytes 1540
  463.6 5.6 %copy-start = (f32[128,16032]{0,1:T(8,128)}, f32[128,16032]{0,1:T(8,128)S(1)}, u32[]{:S(2)}) copy-start(f32[128,16032]{0,1:T(8,128)S(1)} %get-tuple-element.38) | copy-start | bytes 24625156
  485.8 8.0 %copy-start.1 = (f32[128,16032]{0,1:T(8,128)S(1)}, f32[128,16032]{0,1:T(8,128)}, u32[]{:S(2)}) copy-start(f32[128,16032]{0,1:T(8,128)} %copy-done) | copy-start | bytes 24625156
  485.8 8.0 %copy-start.2 = (f32[128]{0:T(128)S(1)}, f32[128]{0:T(128)}, u32[]{:S(2)}) copy-start(f32[128]{0:T(128)} %param.21) | copy-start | bytes 1540
Sparse Core Ops, SparseCore 0:
  10.1 31.8 all-gather.3
  117.4 281.0 reduce-scatter.1
where the time goes:
time: 526 us; the launch traced here: 525 us
  waiting for transfers between devices  314 us (60%)
  blocking collectives  84.1 us (16%)
  other arithmetic  51 us (10%)
  matrix products  43 us (8%)
  local copies, waits for them, and re-layouts  18.8 us (4%)
  between operations  14.1 us (3%)
    reduce_scatter x1, waiting for transfers between devices, on_device(): lax.psum_scatter(jnp.dot(quarter_rows, output_projection_weights, preferr...  281 us
    dot_general x1, matrix products, on_device(): jnp.dot(quarter_rows, output_projection_weights, preferred_element_type=j...  43 us
    all_gather x1, waiting for transfers between devices, on_device(): full_rows = lax.all_gather(final_activation, 'vocab', axis=1, tiled=True)  33 us
    all_to_all x1, blocking collectives, on_device(): lax.all_to_all(full_rows, 'dp', split_axis=1, concat_axis=0, tiled=True)  29.6 us
    psum x1, blocking collectives, on_device(): sample_quantile = lax.psum(partial_quantile, 'vocab')  16.3 us
    reduce_max x1, other arithmetic, on_device(): highest_score = lax.pmax(jnp.max(softened_scores, axis=1), 'vocab')  16.2 us
    pmax x1, blocking collectives, on_device(): highest_score = lax.pmax(jnp.max(softened_scores, axis=1), 'vocab')  16.2 us
    another operation x3, other arithmetic  15.8 us
  transfers between devices with their start and end apart: 2, of which 2 were waited for; matrix products, arithmetic and copies ran while one was open for 0% of the time, Pallas kernels for 0%

commit v1 on v0

v1 whole, which is shorter than its diff:
```python
import functools

import jax
import jax.numpy as jnp
from jax import lax
from jax.experimental import pallas as pl
from jax.experimental.pallas import tpu as pltpu
from jax.sharding import PartitionSpec as P

ROWS = 512
TILE = 128
FINISH_ROWS = 1024
LOWEST = -1e30
SHARES = (5, 11, 11, 5)


def spans(width):
    blocks = pl.cdiv(width, ROWS)
    total, edges, seen = sum(SHARES), [0], 0
    for share in SHARES:
        seen += share
        edge = min(blocks, -(-blocks * seen // total))
        if edge > edges[-1]:
            edges.append(edge)
    return [(low, high) for low, high in zip(edges[:-1], edges[1:])]


def penalize_kernel(
    first_block, width, begins, logits, context, emitted, newest, numbers, *rest
):
    if not begins:
        stats_in, _, _, *rest = rest
    scores, counts, stats = rest
    step = pl.program_id(0)

    @pl.when(step == 0)
    def _():
        if begins:
            stats[0:1, :] = jnp.full_like(stats[0:1, :], LOWEST)
            stats[1:2, :] = jnp.zeros_like(stats[1:2, :])
            stats[2:8, :] = jnp.zeros_like(stats[2:8, :])
        else:
            stats[...] = stats_in[...]

    place = (first_block + step) * ROWS + lax.broadcasted_iota(jnp.int32, (ROWS, TILE), 0)
    first_id = lax.axis_index("vocab") * width
    new_counts = emitted[...] + jnp.where(place + first_id == newest[...], 1, 0)
    counts[...] = new_counts
    raw = logits[...]
    divisor, inverse = numbers[0:1, :], numbers[1:2, :]
    frequency, presence, cooling = numbers[2:3, :], numbers[3:4, :], numbers[4:5, :]
    scale = jnp.where(raw > 0, inverse, divisor)
    value = jnp.where(context[...] + new_counts > 0, raw * scale, raw)
    value = value - frequency * new_counts.astype(jnp.float32)
    value = value - jnp.where(new_counts > 0, presence, 0.0)
    value = value * cooling
    scores[...] = value
    value = jnp.where(place < width, value, LOWEST)
    before = stats[0:1, :]
    highest = jnp.maximum(before, jnp.max(value, axis=0, keepdims=True))
    mass = jnp.sum(jnp.exp(value - highest), axis=0, keepdims=True)
    stats[1:2, :] = stats[1:2, :] * jnp.exp(before - highest) + mass
    stats[0:1, :] = highest


def penalize(low, high, width, logits, context, emitted, newest, numbers, carried):
    lanes = logits.shape[1]
    begins = carried is None
    own = pl.BlockSpec((ROWS, lanes), lambda i: (i, 0))
    shifted = pl.BlockSpec((ROWS, lanes), lambda i: (low + i, 0))
    small = pl.BlockSpec((8, lanes), lambda i: (0, 0))
    line = pl.BlockSpec((1, lanes), lambda i: (0, 0))
    in_specs = [own, shifted, shifted, line, small]
    operands = [logits, context, emitted, newest, numbers]
    aliases = {}
    if not begins:
        anywhere = pl.BlockSpec(memory_space=pl.ANY)
        scores, counts, stats = carried
        in_specs += [small, anywhere, anywhere]
        operands += [stats, scores, counts]
        aliases = {6: 0, 7: 1}
    rows = (high - low) * ROWS
    return pl.pallas_call(
        functools.partial(penalize_kernel, low, width, begins),
        grid=(high - low,),
        in_specs=in_specs,
        out_specs=[shifted, shifted, small],
        out_shape=[
            jax.ShapeDtypeStruct((width, lanes), jnp.float32),
            jax.ShapeDtypeStruct((width, lanes), jnp.int32),
            jax.ShapeDtypeStruct((8, lanes), jnp.float32),
        ],
        input_output_aliases=aliases,
        compiler_params=pltpu.CompilerParams(
            dimension_semantics=("arbitrary",)
        ),
        cost_estimate=pl.CostEstimate(
            flops=rows * lanes * 40,
            bytes_accessed=rows * lanes * 20,
            transcendentals=rows * lanes,
        ),
    )(*operands)


def finish_kernel(width, shards, scores, gathered, draws, likelihoods, quantile, held):
    step = pl.program_id(0)
    own = lax.axis_index("vocab")
    lanes = scores.shape[1]

    @pl.when(step == 0)
    def _():
        highest = gathered[0:1, :]
        for shard in range(1, shards):
            highest = jnp.maximum(highest, gathered[8 * shard : 8 * shard + 1, :])
        total = jnp.zeros_like(highest)
        lower = jnp.zeros_like(highest)
        for shard in range(shards):
            own_highest = gathered[8 * shard : 8 * shard + 1, :]
            mass = gathered[8 * shard + 1 : 8 * shard + 2, :] * jnp.exp(own_highest - highest)
            total = total + mass
            lower = lower + jnp.where(shard < own, mass, 0.0)
        held[0:1, :] = highest
        held[1:2, :] = jnp.log(total)
        held[2:3, :] = lower / total
        quantile[...] = jnp.zeros_like(quantile)

    highest, log_total = held[0:1, :], held[1:2, :]
    draw = draws[...]
    carry = held[2:3, :]
    row = lax.broadcasted_iota(jnp.int32, (TILE, TILE), 0)
    column = lax.broadcasted_iota(jnp.int32, (TILE, TILE), 1)
    strictly_lower = jnp.where(row > column, 1.0, 0.0).astype(jnp.bfloat16)
    spot = lax.broadcasted_iota(jnp.int32, (TILE, lanes), 0)
    first_id = own * width
    gained = jnp.zeros((8, lanes), jnp.float32)
    for tile in range(FINISH_ROWS // TILE):
        base = step * FINISH_ROWS + tile * TILE
        window = slice(tile * TILE, (tile + 1) * TILE)
        value = (scores[window, :] - highest) - log_total
        likelihoods[window, :] = value
        prob = jnp.where(spot < width - base, jnp.exp(value), 0.0)
        below = carry
        left = prob
        for _ in range(3):
            piece = left.astype(jnp.bfloat16)
            left = left - piece.astype(jnp.float32)
            below = below + jnp.dot(
                strictly_lower, piece, preferred_element_type=jnp.float32
            )
        taken = jnp.minimum(jnp.maximum(draw - below, 0.0), prob)
        position = ((spot + (base + first_id)).astype(jnp.float32) + 0.5) * (
            1.0 / (width * shards)
        )
        gained = gained + jnp.sum((taken * position).reshape(TILE // 8, 8, lanes), axis=0)
        carry = carry + jnp.sum(prob, axis=0, keepdims=True)
    held[2:3, :] = carry
    quantile[...] += gained


def finish(scores, gathered, draws, shards):
    width, lanes = scores.shape
    block = pl.BlockSpec((FINISH_ROWS, lanes), lambda i: (i, 0))
    return pl.pallas_call(
        functools.partial(finish_kernel, width, shards),
        grid=(pl.cdiv(width, FINISH_ROWS),),
        in_specs=[
            block,
            pl.BlockSpec((8 * shards, lanes), lambda i: (0, 0)),
            pl.BlockSpec((1, lanes), lambda i: (0, 0)),
        ],
        out_specs=[block, pl.BlockSpec((8, lanes), lambda i: (0, 0))],
        out_shape=[
            jax.ShapeDtypeStruct((width, lanes), jnp.float32),
            jax.ShapeDtypeStruct((8, lanes), jnp.float32),
        ],
        scratch_shapes=[pltpu.VMEM((8, lanes), jnp.float32)],
        compiler_params=pltpu.CompilerParams(
            dimension_semantics=("arbitrary",)
        ),
        cost_estimate=pl.CostEstimate(
            flops=width * lanes * 40,
            bytes_accessed=width * lanes * 8,
            transcendentals=width * lanes,
        ),
    )(scores, gathered, draws)


def quarter_of_features(hidden):
    shards, groups = lax.axis_size("vocab"), lax.axis_size("dp")
    pairs = shards // 2
    same_core = [[core + 2 * pair for pair in range(pairs)] for core in range(2)]
    full_rows = lax.all_gather(
        hidden, "vocab", axis=1, tiled=True, axis_index_groups=same_core
    )
    own = lax.all_to_all(full_rows, "dp", split_axis=1, concat_axis=0, tiled=True)
    other = lax.ppermute(own, "vocab", [(index, index ^ 1) for index in range(shards)])
    shape = (own.shape[0], pairs // groups, 1, hidden.shape[1])
    own, other = own.reshape(shape), other.reshape(shape)
    joined = jnp.where(
        lax.axis_index("vocab") % 2 == 0,
        jnp.concatenate([own, other], 2),
        jnp.concatenate([other, own], 2),
    )
    return joined.reshape(own.shape[0], -1)


def on_device(
    final_activation,
    output_projection_weights,
    context_word_tallies,
    emitted_word_tallies,
    freshest_word,
    recurrence_divisor,
    recurrence_fine,
    appearance_fine,
    softness_level,
    random_draws,
):
    shards = lax.axis_size("vocab")
    width = output_projection_weights.shape[1]
    quarter_rows = quarter_of_features(final_activation)
    numbers = jnp.stack(
        [
            recurrence_divisor,
            1.0 / recurrence_divisor,
            recurrence_fine,
            appearance_fine,
            1.0 / softness_level,
        ]
        + [jnp.zeros_like(softness_level)] * 3
    )
    newest = freshest_word[None, :]
    context, emitted = context_word_tallies.T, emitted_word_tallies.T
    pieces = []
    for low, high in spans(width):
        weights = output_projection_weights[:, low * ROWS : min(high * ROWS, width)]
        share = jnp.dot(quarter_rows, weights, preferred_element_type=jnp.float32)
        pieces.append(
            lax.psum_scatter(share, "dp", scatter_dimension=0, tiled=True)
        )
    carried = None
    for (low, high), piece in zip(spans(width), pieces):
        carried = penalize(
            low, high, width, piece.T, context, emitted, newest, numbers, carried
        )
    scores, new_counts, stats = carried
    gathered = lax.all_gather(stats, "vocab", axis=0, tiled=True)
    likelihoods, parts = finish(scores, gathered, random_draws[None, :], shards)
    part = jnp.sum(parts, axis=0, keepdims=True)
    sample_quantile = jnp.sum(lax.all_gather(part, "vocab", axis=0, tiled=True), axis=0)
    return (new_counts.T, likelihoods.T, sample_quantile)


def solution(mesh):
    return jax.shard_map(
        on_device,
        mesh=mesh,
        in_specs=(
            P("dp", "vocab"),
            P("dp", "vocab"),
            P("dp", "vocab"),
            P("dp", "vocab"),
            P("dp"),
            P("dp"),
            P("dp"),
            P("dp"),
            P("dp"),
            P("dp"),
        ),
        out_specs=(P("dp", "vocab"), P("dp", "vocab"), P("dp")),
        check_vma=False,
    )
```

time: 526 us -> 484 us (0.920)
  Pallas kernels: 0 us -> 48.9 us
  other arithmetic: 51 us -> 3.12 us
  blocking collectives: 84.1 us -> 44.3 us
  matrix products: 43 us -> 61 us
  local copies, waits for them, and re-layouts: 18.8 us -> 6.48 us
  waiting for transfers between devices: 314 us -> 304 us
    pallas_call x0 -> x5, Pallas kernels: none -> 48.9 us  [the longest x4 33.4 us: penalize(): pl.pallas_call(functools.partial(penalize_kernel, low, width, begins), gr...]
    psum x2 -> x0, blocking collectives: 29.9 us -> none  [the longest x1 16.3 us: on_device(): sample_quantile = lax.psum(partial_quantile, 'vocab')]
    all_gather x1 -> x2, blocking collectives: 8.41 us -> 26.9 us  [the longest x1 15.1 us: on_device(): gathered = lax.all_gather(stats, 'vocab', axis=0, tiled=True)]
    dot_general x1 -> x4, matrix products: 43 us -> 61 us  [on_device(): share = jnp.dot(quarter_rows, weights, preferred_element_type=jnp.float32)]
    reduce_max x1 -> x0, other arithmetic: 16.2 us -> none  [on_device(): highest_score = lax.pmax(jnp.max(softened_scores, axis=1), 'vocab')]
    pmax x1 -> x0, blocking collectives: 16.2 us -> none  [on_device(): highest_score = lax.pmax(jnp.max(softened_scores, axis=1), 'vocab')]
    another operation x3 -> x1, other arithmetic: 15.8 us -> 0.01 us  [on_device(): jnp.stack([recurrence_divisor, 1.0 / recurrence_divisor, recurrence_fine,...]
    all_to_all x1, blocking collectives: 29.6 us -> 17.4 us  [quarter_of_features(): lax.all_to_all(full_rows, 'dp', split_axis=1, concat_axis=0, tiled=True)]
  transfers between devices with their start and end apart: 2 -> 6, of which waited for: 2 -> 6; matrix products, arithmetic and copies ran while one was open for 0% -> 10% of each run, Pallas kernels for 0% -> 6%
where the time goes in v1:
time: 484 us; the launch traced here: 482 us
  waiting for transfers between devices  304 us (63%)
  matrix products  61 us (13%)
  Pallas kernels  48.9 us (10%)
  blocking collectives  44.3 us (9%)
  between operations  13.9 us (3%)
  local copies, waits for them, and re-layouts  6.48 us (1%)
    reduce_scatter x4, waiting for transfers between devices, on_device(): lax.psum_scatter(share, 'dp', scatter_dimension=0, tiled=True)  270 us
    dot_general x4, matrix products, on_device(): share = jnp.dot(quarter_rows, weights, preferred_element_type=jnp.float32)  61 us
    pallas_call x4, Pallas kernels, penalize(): pl.pallas_call(functools.partial(penalize_kernel, low, width, begins), gr...  33.4 us
    all_gather x1, waiting for transfers between devices, quarter_of_features(): lax.all_gather(hidden, 'vocab', axis=1, tiled=True, axis_index_groups=sam...  31.8 us
    all_to_all x1, blocking collectives, quarter_of_features(): lax.all_to_all(full_rows, 'dp', split_axis=1, concat_axis=0, tiled=True)  17.4 us
    pallas_call x1, Pallas kernels, finish(): pl.pallas_call(functools.partial(finish_kernel, width, shards), grid=(pl....  15.5 us
    all_gather x1, blocking collectives, on_device(): gathered = lax.all_gather(stats, 'vocab', axis=0, tiled=True)  15.1 us
    all_gather x1, blocking collectives, on_device(): lax.all_gather(part, 'vocab', axis=0, tiled=True)  11.8 us
  transfers between devices with their start and end apart: 6, of which 6 were waited for; matrix products, arithmetic and copies ran while one was open for 10% of the time, Pallas kernels for 6%

profile of v1, /device:TPU:0, one launch (start us, length us, event | category | flops | bytes accessed | tf_op | source)
XLA Modules:
  0.0 482.5 jit_solution(13064394649716536174)
XLA Ops:
  7.2 0.0 all-gather.4.cloned.1.call-start
  7.2 1.8 copy.32
  9.0 0.0 all-gather.4.cloned.1.call-update
  9.0 0.0 reduce-scatter.11.cloned.1.call-start
  9.1 31.8 %all-gather.4.cloned.1.call-done = bf16[128,4096]{0,1:T(8,128)(2,1)} async-done(((bf16[128,1024]{0,1:T(8,128)(2,1)}), bf16[128,4096]{0,1:T(8,128)(2,1)}) %all-gather.4.cloned.1.call-update) | async-done | bytes 1048592 | tf_op jit(solution)/shard_map/all_gather | solution.py:192
  40.9 17.4 %all_to_all.19 = bf16[128,4,1024]{0,2,1:T(8,128)(2,1)S(1)} all-to-all(bf16[128,4,1024]{0,2,1:T(8,128)(2,1)} %bitcast.49), channel_id=1, replica_groups=mesh['dp'=4,'vocab'=8] {'dp'}, dimensions={1} | all-to-all | bytes 2097152 | tf_op jit(solution)/shard_map/all_to_all | solution.py:195
  58.3 0.5 copy.33
  58.8 0.1 collective-permute-start
  58.9 2.6 collective-permute-done
  61.5 0.0 copy-start.1
  61.5 1.0 copy-done.1
  62.5 1.9 maximum_select_fusion
  64.4 2.6 copy.35
  67.0 0.0 copy-start
  67.0 11.7 %fusion.4 = f32[512,2560]{0,1:T(8,128)} fusion(bf16[512,2048]{0,1:T(8,128)(2,1)} %bitcast.42, bf16[2048,16032]{0,1:T(8,128)(2,1)} %param.11), kind=kOutput, calls=%fused_computation.4 | convolution fusion | flops 5368709120 | bytes 17825792 | tf_op jit(solution)/shard_map/dot_general | solution.py:237
  78.6 0.0 reduce-scatter.11.cloned.1.call-update
  78.6 0.0 reduce-scatter.9.cloned.1.call-start
  78.7 0.0 copy-done
  78.7 19.1 %fusion = f32[512,5632]{0,1:T(8,128)} fusion(bf16[512,2048]{0,1:T(8,128)(2,1)S(1)} %bitcast.43, bf16[2048,16032]{0,1:T(8,128)(2,1)} %param.11), kind=kOutput, calls=%fused_computation | convolution fusion | flops 11811160064 | bytes 36700160 | tf_op jit(solution)/shard_map/dot_general | solution.py:237
  97.8 0.0 reduce-scatter.9.cloned.1.call-update
  97.8 0.2 reduce-scatter.7.cloned.1.call-start
  98.1 19.5 %fusion.2 = f32[512,5632]{0,1:T(8,128)} fusion(bf16[512,2048]{0,1:T(8,128)(2,1)S(1)} %bitcast.44, bf16[2048,16032]{0,1:T(8,128)(2,1)} %param.11), kind=kOutput, calls=%fused_computation.2 | convolution fusion | flops 11811160064 | bytes 36700160 | tf_op jit(solution)/shard_map/dot_general | solution.py:237
  117.6 0.0 reduce-scatter.7.cloned.1.call-update
  117.6 0.0 copy-start.2
  117.7 0.0 copy-start.5
  117.7 0.0 copy-start.3
  117.7 0.0 copy-start.4
  117.7 0.0 reduce-scatter.5.cloned.1.call-start
  117.7 10.7 %fusion.6 = f32[512,2208]{0,1:T(8,128)} fusion(bf16[512,2048]{0,1:T(8,128)(2,1)S(1)} %bitcast.45, bf16[2048,16032]{0,1:T(8,128)(2,1)} %param.11), kind=kOutput, calls=%fused_computation.6 | convolution fusion | flops 4630511616 | bytes 15663104 | tf_op jit(solution)/shard_map/dot_general | solution.py:237
  128.4 0.0 reduce-scatter.5.cloned.1.call-update
  128.4 0.0 copy-done.2
  128.4 0.0 copy-done.5
  128.5 0.0 copy-done.3
  128.5 0.0 copy-done.4
  128.5 0.6 stack.27.numbers
  129.1 9.4 %reduce-scatter.11.cloned.1.call-done = f32[128,2560]{0,1:T(8,128)} async-done(((f32[512,2560]{0,1:T(8,128)}), f32[128,2560]{0,1:T(8,128)}) %reduce-scatter.11.cloned.1.call-update) | async-done | bytes 1310736 | tf_op jit(solution)/shard_map/reduce_scatter | solution.py:239
  138.5 5.7 %shard_map.121 = (f32[16032,128]{1,0:T(8,128)}, s32[16032,128]{1,0:T(8,128)}, f32[8,128]{1,0:T(8,128)}) custom-call(f32[2560,128]{1,0:T(8,128)} %bitcast.46, s32[16032,128]{1,0:T(8,128)} %bitcast.28, s32[16032,128]{1,0:T(8,128)} %bitcast.32, s32[1,128]{1,0:T(1,128)} %bitcast.50, f32[8,128]{1,0:T(8,128)} %stack.27.numbers), custom_call_target="tpu_custom_call" | custom-call | flops 13107200 | bytes 6553600 | tf_op jit(solution)/shard_map/pallas_call | solution.py:83
  144.2 109.4 %reduce-scatter.9.cloned.1.call-done = f32[128,5632]{0,1:T(8,128)} async-done(((f32[512,5632]{0,1:T(8,128)}), f32[128,5632]{0,1:T(8,128)}) %reduce-scatter.9.cloned.1.call-update) | async-done | bytes 2883600 | tf_op jit(solution)/shard_map/reduce_scatter | solution.py:239
  253.6 11.1 %shard_map.122 = (f32[16032,128]{1,0:T(8,128)}, s32[16032,128]{1,0:T(8,128)}, f32[8,128]{1,0:T(8,128)}) custom-call(f32[5632,128]{1,0:T(8,128)} %bitcast.41, s32[16032,128]{1,0:T(8,128)} %bitcast.29, s32[16032,128]{1,0:T(8,128)} %bitcast.33, s32[1,128]{1,0:T(1,128)} %bitcast.51, ...), custom_call_target="tpu_custom_call", output_to_operand_aliasing={{0}: (6, {}), {1}: (7, {})} | custom-call | flops 28835840 | bytes 14417920 | tf_op jit(solution)/shard_map/pallas_call | solution.py:83
  264.8 103.9 %reduce-scatter.7.cloned.1.call-done = f32[128,5632]{0,1:T(8,128)} async-done(((f32[512,5632]{0,1:T(8,128)}), f32[128,5632]{0,1:T(8,128)}) %reduce-scatter.7.cloned.1.call-update) | async-done | bytes 2883600 | tf_op jit(solution)/shard_map/reduce_scatter | solution.py:239
  368.7 11.1 %shard_map.123 = (f32[16032,128]{1,0:T(8,128)}, s32[16032,128]{1,0:T(8,128)}, f32[8,128]{1,0:T(8,128)}) custom-call(f32[5632,128]{1,0:T(8,128)} %bitcast.40, s32[16032,128]{1,0:T(8,128)} %bitcast.30, s32[16032,128]{1,0:T(8,128)} %bitcast.34, s32[1,128]{1,0:T(1,128)} %bitcast.52, ...), custom_call_target="tpu_custom_call", output_to_operand_aliasing={{0}: (6, {}), {1}: (7, {})} | custom-call | flops 28835840 | bytes 14417920 | tf_op jit(solution)/shard_map/pallas_call | solution.py:83
  379.8 47.2 %reduce-scatter.5.cloned.1.call-done = f32[128,2208]{0,1:T(8,128)} async-done(((f32[512,2208]{0,1:T(8,128)}), f32[128,2208]{0,1:T(8,128)}) %reduce-scatter.5.cloned.1.call-update) | async-done | bytes 1130512 | tf_op jit(solution)/shard_map/reduce_scatter | solution.py:239
  426.9 5.4 %shard_map.124 = (f32[16032,128]{1,0:T(8,128)}, s32[16032,128]{1,0:T(8,128)}, f32[8,128]{1,0:T(8,128)}) custom-call(f32[2208,128]{1,0:T(8,128)} %bitcast.47, s32[16032,128]{1,0:T(8,128)} %bitcast.31, s32[16032,128]{1,0:T(8,128)} %bitcast.35, s32[1,128]{1,0:T(1,128)} %bitcast.53, ...), custom_call_target="tpu_custom_call", output_to_operand_aliasing={{0}: (6, {}), {1}: (7, {})} | custom-call | flops 13107200 | bytes 6553600 | tf_op jit(solution)/shard_map/pallas_call | solution.py:83
  432.3 15.1 %all_gather.10.gathered = f32[64,128]{1,0:T(8,128)} all-gather(f32[8,128]{1,0:T(8,128)} %get-tuple-element.28), channel_id=1, replica_groups=mesh['dp'=4,'vocab'=8] {'vocab'}, dimensions={0}, use_global_device_ids=true | all-gather | bytes 36864 | tf_op jit(solution)/shard_map/all_gather | solution.py:247
  447.4 15.5 %shard_map.125 = (f32[16032,128]{1,0:T(8,128)}, f32[8,128]{1,0:T(8,128)}) custom-call(f32[16032,128]{1,0:T(8,128)} %get-tuple-element.27.scores, f32[64,128]{1,0:T(8,128)} %all_gather.10.gathered, f32[1,128]{1,0:T(1,128)} %bitcast.56), custom_call_target="tpu_custom_call" | custom-call | flops 82083840 | bytes 16416768 | tf_op jit(solution)/shard_map/pallas_call | solution.py:163
  462.9 0.7 reduce_sum.18
  463.6 11.8 %all-gather.1 = f32[8,1,128]{2,1,0:T(1,128)S(1)} all-gather(f32[1,1,128]{2,1,0:T(1,128)S(1)} %bitcast.54), channel_id=2, replica_groups=mesh['dp'=4,'vocab'=8] {'vocab'}, dimensions={0}, use_global_device_ids=true | all-gather | bytes 4608 | tf_op jit(solution)/shard_map/all_gather | solution.py:250
  475.4 0.5 reduce_sum.19
  (3 shorter events, 0.0 us)
Async XLA Ops:
  7.2 33.7 %all-gather.4.cloned.1.call-start = ((), (), s32[]{:S(2)}) async-start(), calls=%async_computation.5 | async-start | bytes 1310720 | tf_op jit(solution)/shard_map/all_gather | solution.py:192
  9.0 129.5 %reduce-scatter.11.cloned.1.call-start = ((), (), s32[]{:S(2)}) async-start(), calls=%async_computation.9 | async-start | bytes 6553600 | tf_op jit(solution)/shard_map/reduce_scatter | solution.py:239
  58.8 2.7 collective-permute-start
  61.5 1.0 copy-start.1
  67.0 11.7 %copy-start = (bf16[512,1,2,1024]{0,3,2,1:T(8,128)(2,1)S(1)}, bf16[512,1,2,1024]{0,3,2,1:T(8,128)(2,1)}, u32[]{:S(2)}) copy-start(bf16[512,1,2,1024]{0,3,2,1:T(8,128)(2,1)} %copy.35) | copy-start | bytes 6291460
  78.6 175.0 %reduce-scatter.9.cloned.1.call-start = ((), (), s32[]{:S(2)}) async-start(), calls=%async_computation.8 | async-start | bytes 14417920 | tf_op jit(solution)/shard_map/reduce_scatter | solution.py:239
  97.8 270.8 %reduce-scatter.7.cloned.1.call-start = ((), (), s32[]{:S(2)}) async-start(), calls=%async_computation.7 | async-start | bytes 14417920 | tf_op jit(solution)/shard_map/reduce_scatter | solution.py:239
  117.6 10.8 %copy-start.2 = (f32[128]{0:T(128)S(1)}, f32[128]{0:T(128)}, u32[]{:S(2)}) copy-start(f32[128]{0:T(128)} %param.15) | copy-start | bytes 1540
  117.7 10.8 %copy-start.5 = (f32[128]{0:T(128)S(1)}, f32[128]{0:T(128)}, u32[]{:S(2)}) copy-start(f32[128]{0:T(128)} %param.18) | copy-start | bytes 1540
  117.7 10.8 %copy-start.3 = (f32[128]{0:T(128)S(1)}, f32[128]{0:T(128)}, u32[]{:S(2)}) copy-start(f32[128]{0:T(128)} %param.16) | copy-start | bytes 1540
  117.7 10.8 %copy-start.4 = (f32[128]{0:T(128)S(1)}, f32[128]{0:T(128)}, u32[]{:S(2)}) copy-start(f32[128]{0:T(128)} %param.17) | copy-start | bytes 1540
  117.7 309.2 %reduce-scatter.5.cloned.1.call-start = ((), (), s32[]{:S(2)}) async-start(), calls=%async_computation.6 | async-start | bytes 5652480 | tf_op jit(solution)/shard_map/reduce_scatter | solution.py:239
Sparse Core Ops, SparseCore 0:
  10.1 30.6 all-gather.3
  78.8 59.6 reduce-scatter.10
  141.6 112.0 reduce-scatter.8
  256.6 112.0 reduce-scatter.6
  371.6 55.3 reduce-scatter.4
